TPU v7x, 32 devices: a whole 2x2x4 slice. The times are simulated.
32 devices in a mesh: seq: 2 (over x), mp: 4 (over y, core), dp: 4 (over z).
Axes of the slice: x: 2, y: 2, z: 4, core: 2. Of those that a mesh axis runs over, the one named last changes fastest.
Arguments:
- tokens: bfloat16 [16384, 2048], P(('dp', 'seq'), 'mp'), parts along dimension 0, may hold values from -6 to 6
- w_query: bfloat16 [2048, 2048], P(None, 'mp'), may hold values from -0.125 to 0.125
- w_key: bfloat16 [2048, 2048], P(None, 'mp'), may hold values from -0.125 to 0.125
- w_value: bfloat16 [2048, 2048], P(None, 'mp'), may hold values from -0.125 to 0.125
- w_gate: bfloat16 [2048, 2048], P(None, 'mp'), may hold values from -0.125 to 0.125
- decay_exponent: int32 [16], P('mp'), may hold values from 5 to 16
- forget: float32 [16384, 16], P(('dp', 'seq'), 'mp'), parts along dimension 0, may hold values from 0 to 0.69
- norm_gain: float32 [2048], replicated, may hold values from 0.1 to 1.9
Outputs:
- retained: bfloat16 [16384, 2048], P(('dp', 'seq', 'mp')), parts along dimension 0
There are 4 independent parts, one for each index of `dp`. A program takes and returns all parts, laid end to end along the dimension named above; an argument that names none is the same for every part. Nothing has to cross between parts.
All inputs are finite; a program needn't handle non-finite values.
Results may differ from a plain program's by a relative error of at most 0.015.
Values may be sent and summed in bfloat16 or wider, within the bound.
No kernel may reach another device: no remote copies, remote signals or barrier semaphores. Data moves between devices by JAX's collectives and lax.ppermute only.
A program may use at most 64 MiB of HBM per device.

v0:
```python
import jax
import jax.numpy as jnp
from jax import lax
from jax.sharding import PartitionSpec as P

DH = 128


def carried_in(shard, axis, join, neutral):
    place = lax.axis_index(axis)
    gathered = jax.tree.map(
        lambda a, kind: lax.all_gather(a.astype(kind), axis), shard, (jnp.bfloat16, jnp.bfloat16)
    )
    state = jax.tree.map(lambda a, e: jnp.zeros_like(a) + jnp.asarray(e, a.dtype), shard, neutral)

    def one(hop, state):
        return join(
            state,
            jax.tree.map(
                lambda a, own: lax.dynamic_index_in_dim(a, hop, 0, False).astype(own.dtype),
                gathered,
                shard,
            ),
        )

    return lax.fori_loop(0, place, one, state)


def run_blocks(queries, key_rows, values, logdecay, head_count, head_width):
    seq_rows = queries.shape[0]
    block_rows = 512
    block_count = seq_rows // block_rows

    def shaped(source):
        return source.reshape(block_count, block_rows, head_count, head_width)

    decays = logdecay.reshape(block_count, block_rows, head_count)
    position = lax.broadcasted_iota(jnp.int32, (block_rows, block_rows), 0)
    earlier = lax.broadcasted_iota(jnp.int32, (block_rows, block_rows), 1)
    causal = position >= earlier

    def advance(carried, pieces):
        kv_state, offset = carried
        query_blk, key_blk, value_blk, decay_blk = pieces
        running = jnp.cumsum(decay_blk, axis=0)
        heads_first = running.T
        log_gap = heads_first[:, :, None] - heads_first[:, None, :]
        decay_mask = jnp.where(causal[None], jnp.exp(jnp.where(causal[None], log_gap, 0.0)), 0.0)
        scores = jnp.einsum("tha,sha->hts", query_blk, key_blk, preferred_element_type=jnp.float32)
        scores = (scores * decay_mask).astype(jnp.bfloat16)
        inner = jnp.einsum("hts,shb->thb", scores, value_blk, preferred_element_type=jnp.float32)
        query_float = query_blk.astype(jnp.float32)
        earlier_part = jnp.einsum(
            "tha,hab->thb",
            query_float * jnp.exp(running)[:, :, None],
            kv_state,
            precision=lax.Precision.HIGHEST,
        )
        query_device = query_float * jnp.exp(running + offset[None, :])[:, :, None]
        key_scaled = key_blk.astype(jnp.float32) * jnp.exp(running[-1:] - running)[:, :, None]
        kv_state = jnp.exp(running[-1])[:, None, None] * kv_state + jnp.einsum(
            "sha,shb->hab",
            key_scaled,
            value_blk.astype(jnp.float32),
            precision=lax.Precision.HIGHEST,
        )
        return ((kv_state, offset + running[-1]), (inner + earlier_part, query_device))

    initial = (
        jnp.zeros((head_count, head_width, head_width), jnp.float32),
        jnp.zeros((head_count,), jnp.float32),
    )
    final, outputs = lax.scan(
        advance, initial, (shaped(queries), shaped(key_rows), shaped(values), decays)
    )
    local_part = outputs[0].reshape(seq_rows, head_count, head_width)
    query_device = outputs[1].reshape(seq_rows, head_count, head_width)
    return (local_part, query_device, final[0], final[1])


def combine_states(before, after):
    return (before[0] * after[0], after[0][:, None, None] * before[1] + after[1])


def body(tokens, w_query, w_key, w_value, w_gate, decay_exponent, forget, norm_gain):
    seq_rows = tokens.shape[0]
    local_width = w_query.shape[1]
    head_count = decay_exponent.shape[0]
    head_width = local_width // head_count
    empty = jnp.zeros((seq_rows, local_width), jnp.float32)
    summed = (empty, empty, empty, empty)
    piece = lax.all_gather(tokens, "mp", axis=1, tiled=True)
    results = []
    for weight, partial_value in zip((w_query, w_key, w_value, w_gate), summed):
        results.append(jnp.dot(piece, weight, preferred_element_type=jnp.float32))
    projected = tuple(results)
    queries = projected[0].astype(jnp.bfloat16)
    key_rows = (projected[1] * DH ** (-0.5)).astype(jnp.bfloat16)
    values = projected[2].astype(jnp.bfloat16)
    gate = projected[3].astype(jnp.bfloat16)
    rate = jnp.log1p(-jnp.exp2(-decay_exponent.astype(jnp.float32)))
    logdecay = rate[None, :] - forget
    local_part, query_device, own_state, own_total = run_blocks(
        queries, key_rows, values, logdecay, head_count, head_width
    )
    prefix = carried_in(
        (jnp.exp(own_total), own_state),
        "seq",
        combine_states,
        (jnp.ones_like(own_total), jnp.zeros_like(own_state)),
    )
    incoming = prefix[1]
    from_before = jnp.einsum(
        "tha,hab->thb", query_device, incoming, precision=lax.Precision.HIGHEST
    )
    output = (local_part + from_before).astype(jnp.bfloat16).reshape(seq_rows, local_width)
    moved_output, moved_gate = (
        lax.all_to_all(output, "mp", split_axis=0, concat_axis=1, tiled=True),
        lax.all_to_all(gate, "mp", split_axis=0, concat_axis=1, tiled=True),
    )
    output_float = moved_output.astype(jnp.float32)
    rstd = lax.rsqrt(jnp.mean(output_float * output_float, axis=1) + 1e-06)
    gated = (
        jax.nn.silu(moved_gate.astype(jnp.float32))
        * output_float
        * rstd[:, None]
        * norm_gain[None, :]
    )
    return gated.astype(jnp.bfloat16)


def solution(mesh):
    placed = (
        P(("dp", "seq"), "mp"),
        P(None, "mp"),
        P(None, "mp"),
        P(None, "mp"),
        P(None, "mp"),
        P("mp"),
        P(("dp", "seq"), "mp"),
        P(),
    )
    return jax.shard_map(
        body, mesh=mesh, in_specs=placed, out_specs=P(("dp", "seq", "mp"), None), check_vma=False
    )
```

profile of v0, /device:TPU:0, one launch (start us, length us, event | category | flops | bytes accessed | tf_op | source)
XLA Modules:
  0.0 337.5 jit_solution(5486481289894038509)
XLA Ops:
  10.7 59.2 %all-gather.4.cloned.1.call-done = bf16[2048,2048]{1,0:T(8,128)(2,1)} async-done(((bf16[2048,512]{1,0:T(8,128)(2,1)}), bf16[2048,2048]{1,0:T(8,128)(2,1)}) %all-gather.4.cloned.1.call-update) | async-done | bytes 8388624 | tf_op jit(solution)/shard_map/all_gather | solution.py:92
  69.9 9.1 %convolution_convert_fusion = bf16[2048,512]{1,0:T(8,128)(2,1)} fusion(bf16[2048,2048]{1,0:T(8,128)(2,1)} %all-gather.4.cloned.1.call-done, bf16[2048,512]{1,0:T(8,128)(2,1)S(1)} %copy-done), kind=kOutput, calls=%fused_computation.48 | convolution fusion | flops 4296015872 | bytes 12582912 | tf_op jit(solution)/shard_map/dot_general | solution.py:95
  79.0 4.0 %reshape.90 = bf16[4,512,4,128]{3,2,1,0:T(4,128)(2,1)} reshape(bf16[2048,512]{1,0:T(8,128)(2,1)} %convolution_convert_fusion) | data formatting | bytes 4194304 | tf_op jit(solution)/shard_map/reshape | solution.py:35
  83.0 8.5 %convolution_convert_fusion.1 = bf16[2048,512]{1,0:T(8,128)(2,1)S(1)} fusion(bf16[2048,2048]{1,0:T(8,128)(2,1)} %all-gather.4.cloned.1.call-done, bf16[2048,512]{1,0:T(8,128)(2,1)} %param.15), kind=kOutput, calls=%fused_computation.49 | convolution fusion | flops 4296015872 | bytes 12582912 | tf_op jit(solution)/shard_map/dot_general | solution.py:95
  91.5 2.1 reshape.89
  93.6 8.5 %multiply_convert_fusion.2 = bf16[2048,512]{1,0:T(8,128)(2,1)S(1)} fusion(bf16[2048,2048]{1,0:T(8,128)(2,1)} %all-gather.4.cloned.1.call-done, bf16[2048,512]{1,0:T(8,128)(2,1)} %param.14), kind=kOutput, calls=%fused_computation.47 | convolution fusion | flops 4297064448 | bytes 12582912 | tf_op jit(solution)/shard_map/dot_general | solution.py:95
  102.1 2.0 reshape.88
  104.1 137.0 %while.31 = (s32[]{:T(128)}, f32[4,128,128]{2,1,0:T(8,128)S(1)}, f32[4]{0:T(128)S(1)}, f32[4,512,4,128]{1,0,3,2:T(4,128)}, f32[4,512,4,128]{3,1,0,2:T(8,128)}, /...) while((s32[]{:T(128)}, f32[4,128,128]{2,1,0:T(8,128)S(1)}, ...), condition=%wide.region_3.4_spmd.clone.clone, body=%wide.region_0.3_spmd.clone.clone.sunk | while | flops 1350045696 | bytes 18760368 | solution.py:73
  109.1 2.0 fusion.48
  112.5 2.4 convolution_add_fusion.2
  116.0 21.0 %dynamic_update_slice.15 = f32[4,512,4,128]{1,0,3,2:T(4,128)} dynamic-update-slice(f32[4,512,4,128]{1,0,3,2:T(4,128)} %get-tuple-element.371, f32[1,512,4,128]{1,0,3,2:T(1,128)S(1)} %copy.143, s32[]{:T(128)S(6)} %copy.151, s32[]{:T(128)} %constant.52.clone.1..sunk.1, s32[]{:T(128)} %constant.52.clone.1..sunk.1, s32[]{:T(128)} %constant.52.clone.1..sunk.1) | dynamic-update-slice | bytes 2097156 | tf_op jit(solution)/shard_map/while/body/jit(dynamic_update_index_in_dim)/dynamic_update_slice | solution.py:73
  146.7 2.4 convolution_add_fusion.2
  150.2 21.0 %dynamic_update_slice.15 = f32[4,512,4,128]{1,0,3,2:T(4,128)} dynamic-update-slice(f32[4,512,4,128]{1,0,3,2:T(4,128)} %get-tuple-element.371, f32[1,512,4,128]{1,0,3,2:T(1,128)S(1)} %copy.143, s32[]{:T(128)S(6)} %copy.151, s32[]{:T(128)} %constant.52.clone.1..sunk.1, s32[]{:T(128)} %constant.52.clone.1..sunk.1, s32[]{:T(128)} %constant.52.clone.1..sunk.1) | dynamic-update-slice | bytes 2097156 | tf_op jit(solution)/shard_map/while/body/jit(dynamic_update_index_in_dim)/dynamic_update_slice | solution.py:73
  177.6 2.0 fusion.48
  181.0 2.4 convolution_add_fusion.2
  184.5 21.0 %dynamic_update_slice.15 = f32[4,512,4,128]{1,0,3,2:T(4,128)} dynamic-update-slice(f32[4,512,4,128]{1,0,3,2:T(4,128)} %get-tuple-element.371, f32[1,512,4,128]{1,0,3,2:T(1,128)S(1)} %copy.143, s32[]{:T(128)S(6)} %copy.151, s32[]{:T(128)} %constant.52.clone.1..sunk.1, s32[]{:T(128)} %constant.52.clone.1..sunk.1, s32[]{:T(128)} %constant.52.clone.1..sunk.1) | dynamic-update-slice | bytes 2097156 | tf_op jit(solution)/shard_map/while/body/jit(dynamic_update_index_in_dim)/dynamic_update_slice | solution.py:73
  215.2 2.4 convolution_add_fusion.2
  218.7 21.0 %dynamic_update_slice.15 = f32[4,512,4,128]{1,0,3,2:T(4,128)} dynamic-update-slice(f32[4,512,4,128]{1,0,3,2:T(4,128)} %get-tuple-element.371, f32[1,512,4,128]{1,0,3,2:T(1,128)S(1)} %copy.143, s32[]{:T(128)S(6)} %copy.151, s32[]{:T(128)} %constant.52.clone.1..sunk.1, s32[]{:T(128)} %constant.52.clone.1..sunk.1, s32[]{:T(128)} %constant.52.clone.1..sunk.1) | dynamic-update-slice | bytes 2097156 | tf_op jit(solution)/shard_map/while/body/jit(dynamic_update_index_in_dim)/dynamic_update_slice | solution.py:73
  241.4 9.8 %convolution_convert_fusion.2 = bf16[2048,512]{1,0:T(8,128)(2,1)} fusion(bf16[2048,2048]{1,0:T(8,128)(2,1)} %all-gather.4.cloned.1.call-done, bf16[2048,512]{1,0:T(8,128)(2,1)} %param.16), kind=kOutput, calls=%fused_computation.50 | convolution fusion | flops 4296015872 | bytes 12582912 | tf_op jit(solution)/shard_map/dot_general | solution.py:95
  251.2 4.4 %all-to-all-start = ((bf16[4,512,512]{2,1,0:T(8,128)(2,1)}), bf16[4,512,512]{2,1,0:T(8,128)(2,1)}, u32[]{:S(2)}, u32[]{:S(2)}) async-start(bf16[4,512,512]{2,1,0:T(8,128)(2,1)} %bitcast.2), calls=%async_computation | async-start | bytes 4194304 | tf_op jit(solution)/shard_map/all_to_all | solution.py:119
  255.7 4.9 %all-reduce = bf16[8]{0:T(256)(128)(2,1)S(1)} all-reduce(bf16[8]{0:T(256)(128)(2,1)S(1)} %dynamic-update-slice), channel_id=2, replica_groups=mesh['seq'=2,'mp'=4,'dp'=4] {'seq'}, use_global_device_ids=true, to_apply=%add | all-reduce | flops 8 | bytes 32
  260.7 5.7 %all-gather.1 = bf16[8,128,128]{2,1,0:T(8,128)(2,1)S(1)} all-gather(bf16[4,128,128]{2,1,0:T(8,128)(2,1)S(1)} %convert_element_type.89), channel_id=3, replica_groups=mesh['seq'=2,'mp'=4,'dp'=4] {'seq'}, dimensions={0}, use_global_device_ids=true | all-gather | bytes 393216 | tf_op jit(solution)/shard_map/all_gather | solution.py:12
  266.4 6.1 %reshape.91 = f32[2048,4,128]{0,2,1:T(8,128)} reshape(f32[4,512,4,128]{1,0,3,2:T(4,128)} %get-tuple-element.107) | data formatting | bytes 8388608 | tf_op jit(solution)/shard_map/reshape | solution.py:76
  272.5 8.8 %fusion.24 = bf16[2048,4,128]{0,2,1:T(8,128)(2,1)} fusion(f32[2048,4,128]{0,2,1:T(8,128)} %reshape.91, f32[4,128,128]{2,1,0:T(8,128)S(1)} %get-tuple-element.110, f32[2048,4,128]{2,0,1:T(8,128)} %bitcast.128), kind=kOutput, calls=%fused_computation.43 | convolution fusion | flops 1612709888 | bytes 10747904 | tf_op jit(solution)/shard_map/tha,hab->thb/dot_general | solution.py:113
  281.4 3.3 all_to_all.22
  286.4 3.6 %all-to-all-start.1 = ((bf16[4,512,512]{1,2,0:T(8,128)(2,1)}), bf16[4,512,512]{1,2,0:T(8,128)(2,1)S(1)}, u32[]{:S(2)}, u32[]{:S(2)}) async-start(bf16[4,512,512]{1,2,0:T(8,128)(2,1)} %copy.79), calls=%async_computation.1 | async-start | bytes 4194304 | tf_op jit(solution)/shard_map/all_to_all | solution.py:118
  290.0 2.2 convert_bitcast_fusion
  292.2 2.6 copy.94
  294.8 20.9 %all-to-all-done.1 = bf16[4,512,512]{1,2,0:T(8,128)(2,1)S(1)} async-done(((bf16[4,512,512]{1,2,0:T(8,128)(2,1)}), bf16[4,512,512]{1,2,0:T(8,128)(2,1)S(1)}, u32[]{:S(2)}, u32[]{:S(2)}) %all-to-all-start.1) | async-done | bytes 2097184 | tf_op jit(solution)/shard_map/all_to_all | solution.py:118
  316.2 2.6 convert_element_type.105
  318.8 5.4 %copy.80 = f32[512,2048]{1,0:T(8,128)} copy(f32[512,2048]{0,1:T(8,128)} %bitcast.127) | data formatting | bytes 8388608 | tf_op jit(solution)/shard_map/convert_element_type | solution.py:121
  324.2 6.4 %multiply_convert_fusion.1 = bf16[512,2048]{1,0:T(8,128)(2,1)} fusion(f32[512,2048]{1,0:T(8,128)} %copy.80, f32[512,2048]{1,0:T(8,128)} %bitcast.126, f32[2048]{0:T(1024)S(1)} %copy-done.3, f32[512]{0:T(512)S(1)} %add_rsqrt_fusion), kind=kLoop, calls=%fused_computation.45 | loop fusion | flops 8388608 | bytes 10496000 | tf_op jit(solution)/shard_map/convert_element_type | solution.py:129
  (100 shorter events, 45.1 us)
Async XLA Ops:
  6.5 63.4 %copy-start = (bf16[2048,512]{1,0:T(8,128)(2,1)S(1)}, bf16[2048,512]{1,0:T(8,128)(2,1)}, u32[]{:S(2)}) copy-start(bf16[2048,512]{1,0:T(8,128)(2,1)} %param.13) | copy-start | bytes 6291460
  6.5 63.4 %all-gather.4.cloned.1.call-start = ((), (), s32[]{:S(2)}) async-start(), calls=%async_computation.2 | async-start | bytes 10485760 | tf_op jit(solution)/shard_map/all_gather | solution.py:92
  107.4 1.8 copy-start.2
  141.6 1.8 copy-start.2
  175.9 1.8 copy-start.2
  210.1 1.8 copy-start.2
  251.2 35.2 %all-to-all-start = ((bf16[4,512,512]{2,1,0:T(8,128)(2,1)}), bf16[4,512,512]{2,1,0:T(8,128)(2,1)}, u32[]{:S(2)}, u32[]{:S(2)}) async-start(bf16[4,512,512]{2,1,0:T(8,128)(2,1)} %bitcast.2), calls=%async_computation | async-start | bytes 4194304 | tf_op jit(solution)/shard_map/all_to_all | solution.py:119
  286.4 29.3 %all-to-all-start.1 = ((bf16[4,512,512]{1,2,0:T(8,128)(2,1)}), bf16[4,512,512]{1,2,0:T(8,128)(2,1)S(1)}, u32[]{:S(2)}, u32[]{:S(2)}) async-start(bf16[4,512,512]{1,2,0:T(8,128)(2,1)} %copy.79), calls=%async_computation.1 | async-start | bytes 4194304 | tf_op jit(solution)/shard_map/all_to_all | solution.py:118
  318.8 5.4 %copy-start.3 = (f32[2048]{0:T(1024)S(1)}, f32[2048]{0:T(1024)}, u32[]{:S(2)}) copy-start(f32[2048]{0:T(1024)} %param.19) | copy-start | bytes 24580
  324.2 6.4 %copy-start.1 = (bf16[2048,512]{1,0:T(8,128)(2,1)S(1)}, bf16[2048,512]{1,0:T(8,128)(2,1)}, u32[]{:S(2)}) copy-start(bf16[2048,512]{1,0:T(8,128)(2,1)} %param.13) | copy-start | bytes 6291460
Sparse Core Ops, SparseCore 0:
  8.9 60.9 all-gather.3
where the time goes:
time: 341 us; the launch traced here: 337 us
  local copies, waits for them, and re-layouts  131 us (38%)
  waiting for transfers between devices  80.8 us (24%)
  matrix products  67.6 us (20%)
  other arithmetic  25.1 us (7%)
  between operations  14.2 us (4%)
  blocking collectives  10.7 us (3%)
  starting transfers between devices  8.06 us (2%)
    dynamic_update_slice x8, local copies, waits for them, and re-layouts, run_blocks(): lax.scan(advance, initial, (shaped(queries), shaped(key_rows), shaped(val...  88.5 us
    all_gather x1, waiting for transfers between devices, body(): piece = lax.all_gather(tokens, 'mp', axis=1, tiled=True)  59.2 us
    dot_general x4, matrix products, body(): results.append(jnp.dot(piece, weight, preferred_element_type=jnp.float32))  35.9 us
    all_to_all x1, waiting for transfers between devices, body(): lax.all_to_all(output, 'mp', split_axis=0, concat_axis=1, tiled=True)  20.9 us
    dynamic_slice x8, local copies, waits for them, and re-layouts, run_blocks(): lax.scan(advance, initial, (shaped(queries), shaped(key_rows), shaped(val...  11.9 us
    dot_general x4, matrix products, advance(): jnp.einsum('sha,shb->hab', key_scaled, value_blk.astype(jnp.float32), pre...  9.56 us
    dot_general x1, matrix products, body(): jnp.einsum('tha,hab->thb', query_device, incoming, precision=lax.Precisio...  8.83 us
    reshape x3, local copies, waits for them, and re-layouts, shaped(): return source.reshape(block_count, block_rows, head_count, head_width)  8.09 us
  transfers between devices with their start and end apart: 3, of which 2 were waited for; matrix products, arithmetic and copies ran while one was open for 7% of the time, Pallas kernels for 0%

commit v1 on v0

--- a/solution.py
+++ b/solution.py
@@ -4,6 +4,12 @@
 from jax.sharding import PartitionSpec as P
 
 DH = 128
+
+
+def swap_blocks(x, mesh_axis, split, join):
+    cells = jnp.split(x, lax.axis_size(mesh_axis), axis=split)
+    incoming = lax.all_to_all(jnp.stack(cells), mesh_axis, 0, 0)
+    return jnp.concatenate(incoming, axis=join)
 
 
 def carried_in(shard, axis, join, neutral):
@@ -115,7 +121,7 @@
     )
     output = (local_part + from_before).astype(jnp.bfloat16).reshape(seq_rows, local_width)
     moved_output, moved_gate = (
-        lax.all_to_all(output, "mp", split_axis=0, concat_axis=1, tiled=True),
+        swap_blocks(output, "mp", 0, 1),
         lax.all_to_all(gate, "mp", split_axis=0, concat_axis=1, tiled=True),
     )
     output_float = moved_output.astype(jnp.float32)

time: 341 us -> 336 us (0.985)
  local copies, waits for them, and re-layouts: 131 us -> 126 us
    all_to_all x2 -> x0, local copies, waits for them, and re-layouts: 5.04 us -> none  [body(): lax.all_to_all(output, 'mp', split_axis=0, concat_axis=1, tiled=True)]
    another operation x10 -> x11, other arithmetic: 5.59 us -> 7.17 us
where the time goes in v1:
time: 336 us; the launch traced here: 333 us
  local copies, waits for them, and re-layouts  126 us (38%)
  waiting for transfers between devices  80.8 us (24%)
  matrix products  66.3 us (20%)
  other arithmetic  26.7 us (8%)
  between operations  14.2 us (4%)
  blocking collectives  10.7 us (3%)
  starting transfers between devices  8.06 us (2%)
    dynamic_update_slice x8, local copies, waits for them, and re-layouts, run_blocks(): lax.scan(advance, initial, (shaped(queries), shaped(key_rows), shaped(val...  88.5 us
    all_gather x1, waiting for transfers between devices, body(): piece = lax.all_gather(tokens, 'mp', axis=1, tiled=True)  59.2 us
    dot_general x4, matrix products, body(): results.append(jnp.dot(piece, weight, preferred_element_type=jnp.float32))  35.9 us
    all_to_all x1, waiting for transfers between devices, swap_blocks(): incoming = lax.all_to_all(jnp.stack(cells), mesh_axis, 0, 0)  20.9 us
    dynamic_slice x8, local copies, waits for them, and re-layouts, run_blocks(): lax.scan(advance, initial, (shaped(queries), shaped(key_rows), shaped(val...  11.9 us
    dot_general x4, matrix products, advance(): jnp.einsum('sha,shb->hab', key_scaled, value_blk.astype(jnp.float32), pre...  9.56 us
    reshape x3, local copies, waits for them, and re-layouts, shaped(): return source.reshape(block_count, block_rows, head_count, head_width)  8.09 us
    dot_general x4, matrix products, advance(): jnp.einsum('hts,shb->thb', scores, value_blk, preferred_element_type=jnp....  7.92 us
  transfers between devices with their start and end apart: 3, of which 2 were waited for; matrix products, arithmetic and copies ran while one was open for 7% of the time, Pallas kernels for 0%

profile of v1, /device:TPU:0, one launch (start us, length us, event | category | flops | bytes accessed | tf_op | source)
XLA Modules:
  0.0 333.1 jit_solution(903982858529448653)
XLA Ops:
  10.7 59.2 %all-gather.4.cloned.1.call-done = bf16[2048,2048]{1,0:T(8,128)(2,1)} async-done(((bf16[2048,512]{1,0:T(8,128)(2,1)}), bf16[2048,2048]{1,0:T(8,128)(2,1)}) %all-gather.4.cloned.1.call-update) | async-done | bytes 8388624 | tf_op jit(solution)/shard_map/all_gather | solution.py:98
  69.9 9.1 %convolution_convert_fusion = bf16[2048,512]{1,0:T(8,128)(2,1)} fusion(bf16[2048,2048]{1,0:T(8,128)(2,1)} %all-gather.4.cloned.1.call-done, bf16[2048,512]{1,0:T(8,128)(2,1)S(1)} %copy-done), kind=kOutput, calls=%fused_computation.48 | convolution fusion | flops 4296015872 | bytes 12582912 | tf_op jit(solution)/shard_map/dot_general | solution.py:101
  79.0 4.0 %reshape.96 = bf16[4,512,4,128]{3,2,1,0:T(4,128)(2,1)} reshape(bf16[2048,512]{1,0:T(8,128)(2,1)} %convolution_convert_fusion) | data formatting | bytes 4194304 | tf_op jit(solution)/shard_map/reshape | solution.py:41
  83.0 8.5 %convolution_convert_fusion.1 = bf16[2048,512]{1,0:T(8,128)(2,1)S(1)} fusion(bf16[2048,2048]{1,0:T(8,128)(2,1)} %all-gather.4.cloned.1.call-done, bf16[2048,512]{1,0:T(8,128)(2,1)} %param.15), kind=kOutput, calls=%fused_computation.49 | convolution fusion | flops 4296015872 | bytes 12582912 | tf_op jit(solution)/shard_map/dot_general | solution.py:101
  91.5 2.1 reshape.95
  93.6 8.5 %multiply_convert_fusion.2 = bf16[2048,512]{1,0:T(8,128)(2,1)S(1)} fusion(bf16[2048,2048]{1,0:T(8,128)(2,1)} %all-gather.4.cloned.1.call-done, bf16[2048,512]{1,0:T(8,128)(2,1)} %param.14), kind=kOutput, calls=%fused_computation.47 | convolution fusion | flops 4297064448 | bytes 12582912 | tf_op jit(solution)/shard_map/dot_general | solution.py:101
  102.1 2.0 reshape.94
  104.1 137.0 %while.31 = (s32[]{:T(128)}, f32[4,128,128]{2,1,0:T(8,128)S(1)}, f32[4]{0:T(128)S(1)}, f32[4,512,4,128]{1,0,3,2:T(4,128)}, f32[4,512,4,128]{3,1,0,2:T(8,128)}, /...) while((s32[]{:T(128)}, f32[4,128,128]{2,1,0:T(8,128)S(1)}, ...), condition=%wide.region_3.4_spmd.clone.clone, body=%wide.region_0.3_spmd.clone.clone.sunk | while | flops 1350045696 | bytes 18760368 | solution.py:79
  109.1 2.0 fusion.49
  112.5 2.4 convolution_add_fusion.2
  116.0 21.0 %dynamic_update_slice.15 = f32[4,512,4,128]{1,0,3,2:T(4,128)} dynamic-update-slice(f32[4,512,4,128]{1,0,3,2:T(4,128)} %get-tuple-element.375, f32[1,512,4,128]{1,0,3,2:T(1,128)S(1)} %copy.141, s32[]{:T(128)S(6)} %copy.149, s32[]{:T(128)} %constant.52.clone.1..sunk.1, s32[]{:T(128)} %constant.52.clone.1..sunk.1, s32[]{:T(128)} %constant.52.clone.1..sunk.1) | dynamic-update-slice | bytes 2097156 | tf_op jit(solution)/shard_map/while/body/jit(dynamic_update_index_in_dim)/dynamic_update_slice | solution.py:79
  146.7 2.4 convolution_add_fusion.2
  150.2 21.0 %dynamic_update_slice.15 = f32[4,512,4,128]{1,0,3,2:T(4,128)} dynamic-update-slice(f32[4,512,4,128]{1,0,3,2:T(4,128)} %get-tuple-element.375, f32[1,512,4,128]{1,0,3,2:T(1,128)S(1)} %copy.141, s32[]{:T(128)S(6)} %copy.149, s32[]{:T(128)} %constant.52.clone.1..sunk.1, s32[]{:T(128)} %constant.52.clone.1..sunk.1, s32[]{:T(128)} %constant.52.clone.1..sunk.1) | dynamic-update-slice | bytes 2097156 | tf_op jit(solution)/shard_map/while/body/jit(dynamic_update_index_in_dim)/dynamic_update_slice | solution.py:79
  177.6 2.0 fusion.49
  181.0 2.4 convolution_add_fusion.2
  184.5 21.0 %dynamic_update_slice.15 = f32[4,512,4,128]{1,0,3,2:T(4,128)} dynamic-update-slice(f32[4,512,4,128]{1,0,3,2:T(4,128)} %get-tuple-element.375, f32[1,512,4,128]{1,0,3,2:T(1,128)S(1)} %copy.141, s32[]{:T(128)S(6)} %copy.149, s32[]{:T(128)} %constant.52.clone.1..sunk.1, s32[]{:T(128)} %constant.52.clone.1..sunk.1, s32[]{:T(128)} %constant.52.clone.1..sunk.1) | dynamic-update-slice | bytes 2097156 | tf_op jit(solution)/shard_map/while/body/jit(dynamic_update_index_in_dim)/dynamic_update_slice | solution.py:79
  211.9 2.0 fusion.49
  215.2 2.4 convolution_add_fusion.2
  218.7 21.0 %dynamic_update_slice.15 = f32[4,512,4,128]{1,0,3,2:T(4,128)} dynamic-update-slice(f32[4,512,4,128]{1,0,3,2:T(4,128)} %get-tuple-element.375, f32[1,512,4,128]{1,0,3,2:T(1,128)S(1)} %copy.141, s32[]{:T(128)S(6)} %copy.149, s32[]{:T(128)} %constant.52.clone.1..sunk.1, s32[]{:T(128)} %constant.52.clone.1..sunk.1, s32[]{:T(128)} %constant.52.clone.1..sunk.1) | dynamic-update-slice | bytes 2097156 | tf_op jit(solution)/shard_map/while/body/jit(dynamic_update_index_in_dim)/dynamic_update_slice | solution.py:79
  241.4 9.8 %convolution_convert_fusion.2 = bf16[2048,512]{1,0:T(8,128)(2,1)} fusion(bf16[2048,2048]{1,0:T(8,128)(2,1)} %all-gather.4.cloned.1.call-done, bf16[2048,512]{1,0:T(8,128)(2,1)} %param.16), kind=kOutput, calls=%fused_computation.50 | convolution fusion | flops 4296015872 | bytes 12582912 | tf_op jit(solution)/shard_map/dot_general | solution.py:101
  251.2 4.4 %all-to-all-start = ((bf16[4,512,512]{2,1,0:T(8,128)(2,1)}), bf16[4,512,512]{2,1,0:T(8,128)(2,1)}, u32[]{:S(2)}, u32[]{:S(2)}) async-start(bf16[4,512,512]{2,1,0:T(8,128)(2,1)} %bitcast.2), calls=%async_computation | async-start | bytes 4194304 | tf_op jit(solution)/shard_map/all_to_all | solution.py:125
  255.7 4.9 %all-reduce = bf16[8]{0:T(256)(128)(2,1)S(1)} all-reduce(bf16[8]{0:T(256)(128)(2,1)S(1)} %dynamic-update-slice), channel_id=2, replica_groups=mesh['seq'=2,'mp'=4,'dp'=4] {'seq'}, use_global_device_ids=true, to_apply=%add | all-reduce | flops 8 | bytes 32
  260.7 5.7 %all-gather.1 = bf16[8,128,128]{2,1,0:T(8,128)(2,1)S(1)} all-gather(bf16[4,128,128]{2,1,0:T(8,128)(2,1)S(1)} %convert_element_type.89), channel_id=3, replica_groups=mesh['seq'=2,'mp'=4,'dp'=4] {'seq'}, dimensions={0}, use_global_device_ids=true | all-gather | bytes 393216 | tf_op jit(solution)/shard_map/all_gather | solution.py:18
  266.5 6.3 %reshape.97 = f32[2048,4,128]{0,2,1:T(8,128)} reshape(f32[4,512,4,128]{1,0,3,2:T(4,128)} %get-tuple-element.107) | data formatting | bytes 8388608 | tf_op jit(solution)/shard_map/reshape | solution.py:82
  272.8 7.5 %fusion.24 = bf16[2048,4,128]{0,2,1:T(8,128)(2,1)S(1)} fusion(f32[2048,4,128]{0,2,1:T(8,128)} %reshape.97, f32[4,128,128]{2,1,0:T(8,128)S(1)} %get-tuple-element.110, f32[2048,4,128]{2,0,1:T(8,128)} %bitcast.130), kind=kOutput, calls=%fused_computation.43 | convolution fusion | flops 1612709888 | bytes 10747904 | tf_op jit(solution)/shard_map/tha,hab->thb/dot_general | solution.py:119
  282.1 3.6 %all-to-all-start.1 = ((bf16[4,512,512]{1,2,0:T(8,128)(2,1)}), bf16[4,512,512]{1,2,0:T(8,128)(2,1)S(1)}, u32[]{:S(2)}, u32[]{:S(2)}) async-start(bf16[4,512,512]{1,2,0:T(8,128)(2,1)} %pad_maximum_fusion), calls=%async_computation.1 | async-start | bytes 4194304 | tf_op jit(solution)/shard_map/all_to_all | solution.py:11
  285.7 2.2 convert_bitcast_fusion
  287.9 2.6 copy.92
  290.4 20.9 %all-to-all-done.1 = bf16[4,512,512]{1,2,0:T(8,128)(2,1)S(1)} async-done(((bf16[4,512,512]{1,2,0:T(8,128)(2,1)}), bf16[4,512,512]{1,2,0:T(8,128)(2,1)S(1)}, u32[]{:S(2)}, u32[]{:S(2)}) %all-to-all-start.1) | async-done | bytes 2097184 | tf_op jit(solution)/shard_map/all_to_all | solution.py:11
  311.8 2.6 convert_element_type.105
  314.4 5.4 %copy.82 = f32[512,2048]{1,0:T(8,128)} copy(f32[512,2048]{0,1:T(8,128)} %bitcast.129) | data formatting | bytes 8388608 | tf_op jit(solution)/shard_map/convert_element_type | solution.py:127
  319.8 6.4 %multiply_convert_fusion.1 = bf16[512,2048]{1,0:T(8,128)(2,1)} fusion(f32[512,2048]{1,0:T(8,128)} %copy.82, f32[512,2048]{1,0:T(8,128)} %bitcast.128, f32[2048]{0:T(1024)S(1)} %copy-done.3, f32[512]{0:T(512)S(1)} %add_rsqrt_fusion), kind=kLoop, calls=%fused_computation.45 | loop fusion | flops 8388608 | bytes 10496000 | tf_op jit(solution)/shard_map/convert_element_type | solution.py:135
  (100 shorter events, 43.2 us)
Async XLA Ops:
  6.5 63.4 %copy-start = (bf16[2048,512]{1,0:T(8,128)(2,1)S(1)}, bf16[2048,512]{1,0:T(8,128)(2,1)}, u32[]{:S(2)}) copy-start(bf16[2048,512]{1,0:T(8,128)(2,1)} %param.13) | copy-start | bytes 6291460
  6.5 63.4 %all-gather.4.cloned.1.call-start = ((), (), s32[]{:S(2)}) async-start(), calls=%async_computation.2 | async-start | bytes 10485760 | tf_op jit(solution)/shard_map/all_gather | solution.py:98
  107.4 1.8 copy-start.2
  141.6 1.8 copy-start.2
  175.9 1.8 copy-start.2
  210.1 1.8 copy-start.2
  251.2 30.9 %all-to-all-start = ((bf16[4,512,512]{2,1,0:T(8,128)(2,1)}), bf16[4,512,512]{2,1,0:T(8,128)(2,1)}, u32[]{:S(2)}, u32[]{:S(2)}) async-start(bf16[4,512,512]{2,1,0:T(8,128)(2,1)} %bitcast.2), calls=%async_computation | async-start | bytes 4194304 | tf_op jit(solution)/shard_map/all_to_all | solution.py:125
  282.1 29.3 %all-to-all-start.1 = ((bf16[4,512,512]{1,2,0:T(8,128)(2,1)}), bf16[4,512,512]{1,2,0:T(8,128)(2,1)S(1)}, u32[]{:S(2)}, u32[]{:S(2)}) async-start(bf16[4,512,512]{1,2,0:T(8,128)(2,1)} %pad_maximum_fusion), calls=%async_computation.1 | async-start | bytes 4194304 | tf_op jit(solution)/shard_map/all_to_all | solution.py:11
  314.4 5.4 %copy-start.3 = (f32[2048]{0:T(1024)S(1)}, f32[2048]{0:T(1024)}, u32[]{:S(2)}) copy-start(f32[2048]{0:T(1024)} %param.19) | copy-start | bytes 24580
  319.8 6.4 %copy-start.1 = (bf16[2048,512]{1,0:T(8,128)(2,1)S(1)}, bf16[2048,512]{1,0:T(8,128)(2,1)}, u32[]{:S(2)}) copy-start(bf16[2048,512]{1,0:T(8,128)(2,1)} %param.13) | copy-start | bytes 6291460
Sparse Core Ops, SparseCore 0:
  8.9 60.9 all-gather.3
